TPU v7x, 128 devices: a whole 4x4x4 slice. The times are simulated.
128 devices in a mesh: col: 16 (over y, z), row: 8 (over x, core).
Axes of the slice: x: 4, y: 4, z: 4, core: 2. Of those that a mesh axis runs over, the one named last changes fastest.
Arguments:
- u_factors: bfloat16 [2, 64, 256, 64, 128], P(None, 'row', None, 'col'), may hold values from -0.09375 to 0.09375
- v_factors: bfloat16 [2, 64, 256, 64, 128], P(None, 'row', None, 'col'), may hold values from -0.375 to 0.375
- ranks: int32 [2, 64, 64], P(None, 'row', 'col'), may hold values from 8 to 64
- model_init: float32 [2, 16384, 256], P(None, ('col', 'row')), may hold values from -6 to 6
- observed: float32 [2, 16384, 256], P(None, ('row', 'col')), may hold values from -6 to 6
- step: float32 [2], replicated, may hold values from 0.1 to 0.4
Outputs:
- model: float32 [2, 16384, 256], P(None, ('col', 'row'))
- misfit: float32 [2, 16384, 256], P(None, ('row', 'col'))
Inputs may be any that keep to these rules, and one draw needn't show every extreme that they name: `ranks`: columns of a factor beyond its tile's rank do not count.
All inputs are finite; a program needn't handle non-finite values.
Results may differ from a plain program's by a relative error of at most 0.0085.
Values may be sent and summed in bfloat16 or wider, within the bound.
A program may use at most 128 MiB of HBM per device.

v0:
```python
import jax
import jax.numpy as jnp
from jax import lax
from jax.sharding import PartitionSpec as P

ITERS = 2


def split_product(product, rank_mask, rank_most, right_count):
    real = product[..., :rank_most, :right_count] + product[..., rank_most:, right_count:]
    imaginary = product[..., :rank_most, right_count:] - product[..., rank_most:, :right_count]
    weights = rank_mask[..., None]
    return jnp.concatenate([real * weights, imaginary * weights], -1).astype(jnp.bfloat16)


def expand_complex(coefficient, right_count):
    real = coefficient[..., :right_count]
    imaginary = coefficient[..., right_count:]
    upper = jnp.concatenate([real, imaginary], -1)
    lower = jnp.concatenate([-imaginary, real], -1)
    return jnp.concatenate([upper, lower], -2)


def local(u_factors, v_factors, ranks, model_init, observed, step):
    frequencies = model_init.shape[0]
    rank_most = u_factors.shape[-1] // 2
    right_count = model_init.shape[-1] // 2
    tile_size = u_factors.shape[2]
    rows_here = u_factors.shape[1]
    cols_here = u_factors.shape[3]
    rank_mask = (
        jnp.arange(rank_most, dtype=jnp.int32)[None, None, None, :] < ranks[..., None]
    ).astype(jnp.float32)
    model = model_init
    misfit = model_init
    observed_block = lax.all_gather(observed, "col", axis=1, tiled=True)
    for sweep in range(ITERS):
        gathered = lax.all_gather(model.astype(jnp.bfloat16), "row", axis=1, tiled=True)
        model_tiles = gathered.reshape(frequencies, cols_here, tile_size, 2 * right_count)
        product = jnp.einsum(
            "fiajk,fjal->fijkl", v_factors, model_tiles, preferred_element_type=jnp.float32
        )
        coefficient = expand_complex(
            split_product(product, rank_mask, rank_most, right_count), right_count
        )
        partial_value = jnp.einsum(
            "fiajk,fijkl->fial", u_factors, coefficient, preferred_element_type=jnp.float32
        )
        partial_value = partial_value.reshape(frequencies, rows_here * tile_size, 2 * right_count)
        predicted = lax.psum(partial_value, "col")
        full_misfit = predicted - observed_block
        misfit_half = full_misfit.astype(jnp.bfloat16)
        share = observed.shape[1]
        misfit = lax.dynamic_slice_in_dim(full_misfit, lax.axis_index("col") * share, share, 1)
        misfit_tiles = misfit_half.reshape(frequencies, rows_here, tile_size, 2 * right_count)
        product = jnp.einsum(
            "fiajk,fial->fijkl", u_factors, misfit_tiles, preferred_element_type=jnp.float32
        )
        back = expand_complex(
            split_product(product, rank_mask, rank_most, right_count), right_count
        )
        gradient_part = jnp.einsum(
            "fiajk,fijkl->fjal", v_factors, back, preferred_element_type=jnp.float32
        )
        gradient_part = gradient_part.reshape(frequencies, cols_here * tile_size, 2 * right_count)
        gradient = lax.psum_scatter(gradient_part, "row", scatter_dimension=1, tiled=True)
        model = model - step[:, None, None] * gradient
    return (model, misfit)


def solution(mesh):
    return jax.shard_map(
        local,
        mesh=mesh,
        in_specs=(
            P(None, "row", None, "col", None),
            P(None, "row", None, "col", None),
            P(None, "row", "col"),
            P(None, ("col", "row"), None),
            P(None, ("row", "col"), None),
            P(),
        ),
        out_specs=(P(None, ("col", "row"), None), P(None, ("row", "col"), None)),
        check_vma=False,
    )
```

profile of v0, /device:TPU:0, one launch (start us, length us, event | category | flops | bytes accessed | tf_op | source)
XLA Modules:
  0.0 443.3 jit_solution(17294954381206863518)
XLA Ops:
  7.2 1.6 convert_element_type.23
  8.9 7.5 %copy.8 = bf16[2,8,256,4,128]{2,4,1,3,0:T(8,128)(2,1)} copy(bf16[2,8,256,4,128]{4,3,2,1,0:T(4,128)(2,1)} %param.7) | data formatting | bytes 8388608 | tf_op args[1]
  16.4 7.4 %copy.11 = bf16[2,8,256,4,128]{2,4,3,1,0:T(8,128)(2,1)} copy(bf16[2,8,256,4,128]{4,3,2,1,0:T(4,128)(2,1)} %param.6) | data formatting | bytes 8388608 | tf_op args[0]
  23.8 12.1 %all-gather.4.cloned.1.call-done = bf16[2,1024,256]{2,1,0:T(8,128)(2,1)} async-done(((bf16[2,128,256]{2,1,0:T(8,128)(2,1)}), bf16[2,1024,256]{2,1,0:T(8,128)(2,1)}) %all-gather.4.cloned.1.call-update) | async-done | bytes 1048592 | tf_op jit(solution)/shard_map/all_gather | solution.py:38
  36.0 3.7 fusion.49
  39.7 0.8 fusion.47
  41.2 1.5 copy-done
  42.7 2.9 fusion.18
  46.4 103.1 %all-reduce.3.cloned.1.call-done = f32[2,2048,256]{2,1,0:T(8,128)} async-done(((f32[2,2048,256]{2,1,0:T(8,128)}), f32[2,2048,256]{2,1,0:T(8,128)}) %all-reduce.3.cloned.1.call-update) | async-done | bytes 4194320 | tf_op jit(solution)/shard_map/psum | solution.py:50
  149.5 53.4 %all-gather.6.cloned.1.call-done = f32[2,2048,256]{2,1,0:T(8,128)} async-done(((f32[2,128,256]{2,1,0:T(8,128)}), f32[2,2048,256]{2,1,0:T(8,128)}) %all-gather.6.cloned.1.call-update) | async-done | bytes 4194320 | tf_op jit(solution)/shard_map/all_gather | solution.py:36
  202.9 4.3 subtract_convert_fusion
  207.5 1.3 fusion.50
  208.8 1.0 copy.31
  209.8 0.8 fusion.45
  211.3 1.5 copy-done.4
  212.8 2.8 fusion
  215.6 33.5 %reduce-scatter.3.cloned.1.call-done = f32[2,128,256]{2,1,0:T(8,128)} async-done(((f32[2,1024,256]{2,1,0:T(8,128)}), f32[2,128,256]{2,1,0:T(8,128)}) %reduce-scatter.3.cloned.1.call-update) | async-done | bytes 262160 | tf_op jit(solution)/shard_map/reduce_scatter | solution.py:66
  249.1 1.7 fusion.36
  250.9 22.4 %all-gather.8.cloned.1.call-done = bf16[2,1024,256]{2,1,0:T(8,128)(2,1)} async-done(((bf16[2,128,256]{2,1,0:T(8,128)(2,1)}), bf16[2,1024,256]{2,1,0:T(8,128)(2,1)}) %all-gather.8.cloned.1.call-update) | async-done | bytes 1048592 | tf_op jit(solution)/shard_map/all_gather | solution.py:38
  273.3 3.7 fusion.51
  278.6 1.5 copy-done.2
  280.0 2.9 fusion.16
  283.2 103.7 %all-reduce.5.cloned.1.call-done = f32[2,2048,256]{2,1,0:T(8,128)} async-done(((f32[2,2048,256]{2,1,0:T(8,128)}), f32[2,2048,256]{2,1,0:T(8,128)}) %all-reduce.5.cloned.1.call-update) | async-done | bytes 4194320 | tf_op jit(solution)/shard_map/psum | solution.py:50
  386.8 6.2 %fusion.42 = (bf16[2,2048,256]{2,1,0:T(8,128)(2,1)S(1)}, f32[2,2048,256]{2,1,0:T(8,128)}) fusion(f32[2,2048,256]{2,1,0:T(8,128)} %all-reduce.5.cloned.1.call-done, f32[2,2048,256]{2,1,0:T(8,128)} %all-gather.6.cloned.1.call-done), kind=kLoop, calls=%fused_computation.58 | loop fusion | flops 2097152 | bytes 14680064 | tf_op jit(solution)/shard_map/convert_element_type | solution.py:52
  393.0 1.3 fusion.52
  394.3 1.0 copy.30
  395.3 0.8 fusion.40
  396.8 1.5 copy-done.5
  398.3 2.8 fusion.8
  401.1 1.7 constant_dynamic-slice_fusion
  402.7 32.0 %reduce-scatter.5.cloned.1.call-done = f32[2,128,256]{2,1,0:T(8,128)} async-done(((f32[2,1024,256]{2,1,0:T(8,128)}), f32[2,128,256]{2,1,0:T(8,128)}) %reduce-scatter.5.cloned.1.call-update) | async-done | bytes 262160 | tf_op jit(solution)/shard_map/reduce_scatter | solution.py:66
  434.7 1.8 multiply_subtract_fusion
  (36 shorter events, 5.3 us)
Async XLA Ops:
  7.2 28.8 %all-gather.4.cloned.1.call-start = ((), (), s32[]{:S(2)}) async-start(), calls=%async_computation.2 | async-start | bytes 1179648 | tf_op jit(solution)/shard_map/all_gather | solution.py:38
  8.9 140.7 %all-reduce.3.cloned.1.call-start = ((), (), s32[]{:S(2)}) async-start(), calls=%async_computation.3 | async-start | bytes 8388608 | tf_op jit(solution)/shard_map/psum | solution.py:50
  16.4 7.4 %copy-start.8 = (s32[2,8,4]{1,2,0:T(4,128)S(1)}, s32[2,8,4]{1,2,0:T(4,128)}, u32[]{:S(2)}) copy-start(s32[2,8,4]{1,2,0:T(4,128)} %param.8) | copy-start | bytes 772
  40.5 2.2 copy-start
  45.6 157.3 %all-gather.6.cloned.1.call-start = ((), (), s32[]{:S(2)}) async-start(), calls=%async_computation.4 | async-start | bytes 4456448 | tf_op jit(solution)/shard_map/all_gather | solution.py:36
  46.4 202.7 %reduce-scatter.3.cloned.1.call-start = ((), (), s32[]{:S(2)}) async-start(), calls=%async_computation.5 | async-start | bytes 2359296 | tf_op jit(solution)/shard_map/reduce_scatter | solution.py:66
  202.9 4.6 %copy-start.1 = (bf16[2,8,256,4,128]{2,4,3,1,0:T(8,128)(2,1)S(1)}, bf16[2,8,256,4,128]{2,4,3,1,0:T(8,128)(2,1)}, u32[]{:S(2)}) copy-start(bf16[2,8,256,4,128]{2,4,3,1,0:T(8,128)(2,1)} %copy.11) | copy-start | bytes 12582916
  210.6 2.2 copy-start.4
  212.8 36.3 %copy-start.6 = (f32[2,128,256]{2,1,0:T(8,128)S(1)}, f32[2,128,256]{2,1,0:T(8,128)}, u32[]{:S(2)}) copy-start(f32[2,128,256]{2,1,0:T(8,128)} %param.9) | copy-start | bytes 786436
  212.8 36.3 %copy-start.9 = (f32[2]{0:T(128)S(1)}, f32[2]{0:T(128)}, u32[]{:S(2)}) copy-start(f32[2]{0:T(128)} %param.11) | copy-start | bytes 28
  215.6 57.7 %all-gather.8.cloned.1.call-start = ((), (), s32[]{:S(2)}) async-start(), calls=%async_computation.6 | async-start | bytes 1179648 | tf_op jit(solution)/shard_map/all_gather | solution.py:38
  250.8 136.0 %all-reduce.5.cloned.1.call-start = ((), (), s32[]{:S(2)}) async-start(), calls=%async_computation.7 | async-start | bytes 8388608 | tf_op jit(solution)/shard_map/psum | solution.py:50
  277.8 2.2 copy-start.2
  283.0 151.8 %reduce-scatter.5.cloned.1.call-start = ((), (), s32[]{:S(2)}) async-start(), calls=%async_computation.8 | async-start | bytes 2359296 | tf_op jit(solution)/shard_map/reduce_scatter | solution.py:66
  386.8 6.2 %copy-start.3 = (bf16[2,8,256,4,128]{2,4,3,1,0:T(8,128)(2,1)S(1)}, bf16[2,8,256,4,128]{2,4,3,1,0:T(8,128)(2,1)}, u32[]{:S(2)}) copy-start(bf16[2,8,256,4,128]{2,4,3,1,0:T(8,128)(2,1)} %copy.11) | copy-start | bytes 12582916
  396.1 2.2 copy-start.5
  398.3 36.5 %copy-start.7 = (f32[2,128,256]{2,1,0:T(8,128)S(1)}, f32[2,128,256]{2,1,0:T(8,128)}, u32[]{:S(2)}) copy-start(f32[2,128,256]{2,1,0:T(8,128)} %reduce-scatter.3.cloned.1.call-done) | copy-start | bytes 786436
Sparse Core Ops, SparseCore 0:
  10.2 25.6 all-gather.3
  45.7 103.7 all-reduce.2
  151.7 51.1 all-gather.5
  215.7 33.3 reduce-scatter.2
  251.2 22.0 all-gather.7
  283.1 103.7 all-reduce.4
  401.2 33.4 reduce-scatter.4
where the time goes:
time: 444 us; the launch traced here: 443 us
  waiting for transfers between devices  361 us (81%)
  local copies, waits for them, and re-layouts  24.7 us (6%)
  other arithmetic  21.6 us (5%)
  matrix products  21.4 us (5%)
  between operations  14.3 us (3%)
    psum x2, waiting for transfers between devices, local(): predicted = lax.psum(partial_value, 'col')  207 us
    reduce_scatter x2, waiting for transfers between devices, local(): lax.psum_scatter(gradient_part, 'row', scatter_dimension=1, tiled=True)  65.5 us
    all_gather x1, waiting for transfers between devices, local(): observed_block = lax.all_gather(observed, 'col', axis=1, tiled=True)  53.4 us
    all_gather x2, waiting for transfers between devices, local(): lax.all_gather(model.astype(jnp.bfloat16), 'row', axis=1, tiled=True)  34.6 us
    unnamed x22, local copies, waits for them, and re-layouts  21 us
    convert_element_type x2, other arithmetic, local(): misfit_half = full_misfit.astype(jnp.bfloat16)  10.5 us
    unnamed x4, matrix products  9.98 us
  transfers between devices with their start and end apart: 7, of which 7 were waited for; matrix products, arithmetic and copies ran while one was open for 4% of the time, Pallas kernels for 0%

commit v1 on v0

--- a/solution.py
+++ b/solution.py
@@ -47,7 +47,11 @@
             "fiajk,fijkl->fial", u_factors, coefficient, preferred_element_type=jnp.float32
         )
         partial_value = partial_value.reshape(frequencies, rows_here * tile_size, 2 * right_count)
-        predicted = lax.psum(partial_value, "col")
+        predicted = partial_value
+        for hop in (1, 2, 4, 8):
+            predicted = predicted + lax.ppermute(
+                predicted, "col", [(dev, dev ^ hop) for dev in range(16)]
+            )
         full_misfit = predicted - observed_block
         misfit_half = full_misfit.astype(jnp.bfloat16)
         share = observed.shape[1]

time: 444 us -> 958 us (2.16)
  waiting for transfers between devices: 361 us -> 841 us
  starting transfers between devices: 0.47 us -> 19.3 us
  other arithmetic: 21.6 us -> 35.3 us
    ppermute x0 -> x8, waiting for transfers between devices: none -> 741 us  [local(): lax.ppermute(predicted, 'col', [(dev, dev ^ hop) for dev in range(16)])]
    psum x2 -> x0, waiting for transfers between devices: 207 us -> none  [local(): predicted = lax.psum(partial_value, 'col')]
    all_gather x1, waiting for transfers between devices: 53.4 us -> 0.01 us  [local(): observed_block = lax.all_gather(observed, 'col', axis=1, tiled=True)]
    ppermute x0 -> x8, starting transfers between devices: none -> 18.9 us  [local(): lax.ppermute(predicted, 'col', [(dev, dev ^ hop) for dev in range(16)])]
    add x0 -> x6, other arithmetic: none -> 11.7 us  [local(): predicted + lax.ppermute(predicted, 'col', [(dev, dev ^ hop) for dev in r...]
  transfers between devices with their start and end apart: 7 -> 13, of which waited for: 7 -> 12; matrix products, arithmetic and copies ran while one was open for 4% -> 2% of each run, Pallas kernels for 0% -> 0%
where the time goes in v1:
time: 958 us
  waiting for transfers between devices  841 us (88%)
  other arithmetic  35.3 us (4%)
  local copies, waits for them, and re-layouts  26.8 us (3%)
  matrix products  19.8 us (2%)
  starting transfers between devices  19.3 us (2%)
  between operations  15.4 us (2%)
    ppermute x8, waiting for transfers between devices, local(): lax.ppermute(predicted, 'col', [(dev, dev ^ hop) for dev in range(16)])  741 us
    reduce_scatter x2, waiting for transfers between devices, local(): lax.psum_scatter(gradient_part, 'row', scatter_dimension=1, tiled=True)  66 us
    all_gather x2, waiting for transfers between devices, local(): lax.all_gather(model.astype(jnp.bfloat16), 'row', axis=1, tiled=True)  34.6 us
    unnamed x22, local copies, waits for them, and re-layouts  19.8 us
  transfers between devices with their start and end apart: 13, of which 12 were waited for; matrix products, arithmetic and copies ran while one was open for 2% of the time, Pallas kernels for 0%

profile of v1, /device:TPU:0, one launch (start us, length us, event | category | flops | bytes accessed | tf_op | source)
XLA Modules:
  0.0 957.8 jit_solution(15285363197640229625)
XLA Ops:
  9.7 7.5 copy.8
  17.2 7.3 copy.11
  24.6 12.2 %all-gather.4.cloned.1.call-done = bf16[2,1024,256]{2,1,0:T(8,128)(2,1)} async-done(((bf16[2,128,256]{2,1,0:T(8,128)(2,1)}), bf16[2,1024,256]{2,1,0:T(8,128)(2,1)}) %all-gather.4.cloned.1.call-update) | async-done | bytes 1048592 | tf_op jit(solution)/shard_map/all_gather | solution.py:38
  36.8 3.7 fusion.49
  43.5 2.1 fusion.18
  47.3 91.1 %collective-permute-done = f32[2,2048,256]{2,1,0:T(8,128)S(1)} collective-permute-done((f32[2,2048,256]{2,1,0:T(8,128)S(1)}, f32[2,2048,256]{2,1,0:T(8,128)S(1)}, u32[]{:S(2)}, u32[]{:S(2)}) %collective-permute-start) | collective-permute-done | bytes 4194336 | tf_op jit(solution)/shard_map/ppermute | solution.py:52
  139.5 3.2 collective-permute-start.1
  142.7 90.2 %collective-permute-done.1 = f32[2,2048,256]{2,1,0:T(8,128)S(1)} collective-permute-done((f32[2,2048,256]{2,1,0:T(8,128)S(1)}, f32[2,2048,256]{2,1,0:T(8,128)S(1)}, u32[]{:S(2)}, u32[]{:S(2)}) %collective-permute-start.1) | collective-permute-done | bytes 4194336 | tf_op jit(solution)/shard_map/ppermute | solution.py:52
  232.9 2.5 add.45
  237.0 110.8 %collective-permute-done.2 = f32[2,2048,256]{2,1,0:T(8,128)} collective-permute-done((f32[2,2048,256]{2,1,0:T(8,128)}, f32[2,2048,256]{2,1,0:T(8,128)}, u32[]{:S(2)}, u32[]{:S(2)}) %collective-permute-start.2) | collective-permute-done | bytes 4194336 | tf_op jit(solution)/shard_map/ppermute | solution.py:52
  347.8 6.0 add.46
  353.8 3.0 collective-permute-start.3
  356.8 88.9 %collective-permute-done.3 = f32[2,2048,256]{2,1,0:T(8,128)} collective-permute-done((f32[2,2048,256]{2,1,0:T(8,128)}, f32[2,2048,256]{2,1,0:T(8,128)}, u32[]{:S(2)}, u32[]{:S(2)}) %collective-permute-start.3) | collective-permute-done | bytes 4194336 | tf_op jit(solution)/shard_map/ppermute | solution.py:52
  445.7 5.5 subtract_convert_fusion
  456.5 2.8 fusion
  459.4 33.8 %reduce-scatter.3.cloned.1.call-done = f32[2,128,256]{2,1,0:T(8,128)} async-done(((f32[2,1024,256]{2,1,0:T(8,128)}), f32[2,128,256]{2,1,0:T(8,128)}) %reduce-scatter.3.cloned.1.call-update) | async-done | bytes 262160 | tf_op jit(solution)/shard_map/reduce_scatter | solution.py:70
  495.2 22.5 %all-gather.8.cloned.1.call-done = bf16[2,1024,256]{2,1,0:T(8,128)(2,1)} async-done(((bf16[2,128,256]{2,1,0:T(8,128)(2,1)}), bf16[2,1024,256]{2,1,0:T(8,128)(2,1)}) %all-gather.8.cloned.1.call-update) | async-done | bytes 1048592 | tf_op jit(solution)/shard_map/all_gather | solution.py:38
  517.6 3.7 fusion.51
  524.3 2.2 fusion.16
  528.2 91.1 %collective-permute-done.4 = f32[2,2048,256]{2,1,0:T(8,128)S(1)} collective-permute-done((f32[2,2048,256]{2,1,0:T(8,128)S(1)}, f32[2,2048,256]{2,1,0:T(8,128)S(1)}, u32[]{:S(2)}, u32[]{:S(2)}) %collective-permute-start.4) | collective-permute-done | bytes 4194336 | tf_op jit(solution)/shard_map/ppermute | solution.py:52
  620.4 3.2 collective-permute-start.5
  623.6 90.2 %collective-permute-done.5 = f32[2,2048,256]{2,1,0:T(8,128)S(1)} collective-permute-done((f32[2,2048,256]{2,1,0:T(8,128)S(1)}, f32[2,2048,256]{2,1,0:T(8,128)S(1)}, u32[]{:S(2)}, u32[]{:S(2)}) %collective-permute-start.5) | collective-permute-done | bytes 4194336 | tf_op jit(solution)/shard_map/ppermute | solution.py:52
  715.9 89.5 %collective-permute-done.6 = f32[2,2048,256]{2,1,0:T(8,128)S(1)} collective-permute-done((f32[2,2048,256]{2,1,0:T(8,128)S(1)}, f32[2,2048,256]{2,1,0:T(8,128)S(1)}, u32[]{:S(2)}, u32[]{:S(2)}) %collective-permute-start.6) | collective-permute-done | bytes 4194336 | tf_op jit(solution)/shard_map/ppermute | solution.py:52
  806.0 3.1 collective-permute-start.7
  809.1 88.6 %collective-permute-done.7 = f32[2,2048,256]{2,1,0:T(8,128)S(1)} collective-permute-done((f32[2,2048,256]{2,1,0:T(8,128)S(1)}, f32[2,2048,256]{2,1,0:T(8,128)S(1)}, u32[]{:S(2)}, u32[]{:S(2)}) %collective-permute-start.7) | collective-permute-done | bytes 4194336 | tf_op jit(solution)/shard_map/ppermute | solution.py:52
  897.7 2.9 fusion.42
  901.8 4.3 copy.30
  906.1 2.7 fusion.40
  908.7 2.8 fusion.23
  912.3 2.7 fusion.8
  916.7 32.2 %reduce-scatter.5.cloned.1.call-done = f32[2,128,256]{2,1,0:T(8,128)} async-done(((f32[2,1024,256]{2,1,0:T(8,128)}), f32[2,128,256]{2,1,0:T(8,128)}) %reduce-scatter.5.cloned.1.call-update) | async-done | bytes 262160 | tf_op jit(solution)/shard_map/reduce_scatter | solution.py:70
  948.9 1.8 multiply_subtract_fusion
  (52 shorter events, 28.2 us)
Async XLA Ops:
  8.0 28.8 %all-gather.4.cloned.1.call-start = ((), (), s32[]{:S(2)}) async-start(), calls=%async_computation.2 | async-start | bytes 1179648 | tf_op jit(solution)/shard_map/all_gather | solution.py:38
  9.7 347.1 %all-gather.6.cloned.1.call-start = ((), (), s32[]{:S(2)}) async-start(), calls=%async_computation.3 | async-start | bytes 4456448 | tf_op jit(solution)/shard_map/all_gather | solution.py:36
  17.2 7.3 copy-start.8
  41.3 2.2 copy-start
  45.7 92.8 %collective-permute-start = (f32[2,2048,256]{2,1,0:T(8,128)S(1)}, f32[2,2048,256]{2,1,0:T(8,128)S(1)}, u32[]{:S(2)}, u32[]{:S(2)}) collective-permute-start(f32[2,2048,256]{2,1,0:T(8,128)S(1)} %bitcast.79), channel_id=1, source_target_pairs={{0,8},{8,0},{16,24},{24,16},{32,40},{40,32},{48,56},{56,48},{64,72... | collective-permute-start | bytes 12582920 | tf_op jit(solution)/shard_map/ppermute | solution.py:52
  139.5 93.4 %collective-permute-start.1 = (f32[2,2048,256]{2,1,0:T(8,128)S(1)}, f32[2,2048,256]{2,1,0:T(8,128)S(1)}, u32[]{:S(2)}, u32[]{:S(2)}) collective-permute-start(f32[2,2048,256]{2,1,0:T(8,128)S(1)} %bitcast_add_fusion.1), channel_id=1, source_target_pairs={{0,16},{8,24},{16,0},{24,8},{32,48},{40,56},{48,32},{56,40},{64,80... | collective-permute-start | bytes 12582920 | tf_op jit(solution)/shard_map/ppermute | solution.py:52
  235.4 112.4 %collective-permute-start.2 = (f32[2,2048,256]{2,1,0:T(8,128)}, f32[2,2048,256]{2,1,0:T(8,128)}, u32[]{:S(2)}, u32[]{:S(2)}) collective-permute-start(f32[2,2048,256]{2,1,0:T(8,128)} %add.45), channel_id=1, source_target_pairs={{0,32},{8,40},{16,48},{24,56},{32,0},{40,8},{48,16},{56,24},{64,96... | collective-permute-start | bytes 12582920 | tf_op jit(solution)/shard_map/ppermute | solution.py:52
  237.0 256.2 %reduce-scatter.3.cloned.1.call-start = ((), (), s32[]{:S(2)}) async-start(), calls=%async_computation.4 | async-start | bytes 2359296 | tf_op jit(solution)/shard_map/reduce_scatter | solution.py:70
  353.8 91.9 %collective-permute-start.3 = (f32[2,2048,256]{2,1,0:T(8,128)}, f32[2,2048,256]{2,1,0:T(8,128)}, u32[]{:S(2)}, u32[]{:S(2)}) collective-permute-start(f32[2,2048,256]{2,1,0:T(8,128)} %add.46), channel_id=1, source_target_pairs={{0,64},{8,72},{16,80},{24,88},{32,96},{40,104},{48,112},{56,120},{... | collective-permute-start | bytes 12582920 | tf_op jit(solution)/shard_map/ppermute | solution.py:52
  356.8 94.5 %copy-start.1 = (bf16[2,8,256,4,128]{2,4,3,1,0:T(8,128)(2,1)S(1)}, bf16[2,8,256,4,128]{2,4,3,1,0:T(8,128)(2,1)}, u32[]{:S(2)}) copy-start(bf16[2,8,256,4,128]{2,4,3,1,0:T(8,128)(2,1)} %copy.11) | copy-start | bytes 12582916
  454.3 2.2 copy-start.3
  456.5 36.7 %copy-start.6 = (f32[2,128,256]{2,1,0:T(8,128)S(1)}, f32[2,128,256]{2,1,0:T(8,128)}, u32[]{:S(2)}) copy-start(f32[2,128,256]{2,1,0:T(8,128)} %param.9) | copy-start | bytes 786436
  456.5 36.7 %copy-start.9 = (f32[2]{0:T(128)S(1)}, f32[2]{0:T(128)}, u32[]{:S(2)}) copy-start(f32[2]{0:T(128)} %param.11) | copy-start | bytes 28
  459.3 58.3 %all-gather.8.cloned.1.call-start = ((), (), s32[]{:S(2)}) async-start(), calls=%async_computation.5 | async-start | bytes 1179648 | tf_op jit(solution)/shard_map/all_gather | solution.py:38
  494.9 453.9 %reduce-scatter.5.cloned.1.call-start = ((), (), s32[]{:S(2)}) async-start(), calls=%async_computation.6 | async-start | bytes 2359296 | tf_op jit(solution)/shard_map/reduce_scatter | solution.py:70
  522.1 2.2 copy-start.2
  526.5 92.8 %collective-permute-start.4 = (f32[2,2048,256]{2,1,0:T(8,128)S(1)}, f32[2,2048,256]{2,1,0:T(8,128)S(1)}, u32[]{:S(2)}, u32[]{:S(2)}) collective-permute-start(f32[2,2048,256]{2,1,0:T(8,128)S(1)} %bitcast.80), channel_id=1, source_target_pairs={{0,8},{8,0},{16,24},{24,16},{32,40},{40,32},{48,56},{56,48},{64,72... | collective-permute-start | bytes 12582920 | tf_op jit(solution)/shard_map/ppermute | solution.py:52
  620.4 93.4 %collective-permute-start.5 = (f32[2,2048,256]{2,1,0:T(8,128)S(1)}, f32[2,2048,256]{2,1,0:T(8,128)S(1)}, u32[]{:S(2)}, u32[]{:S(2)}) collective-permute-start(f32[2,2048,256]{2,1,0:T(8,128)S(1)} %bitcast_add_fusion), channel_id=1, source_target_pairs={{0,16},{8,24},{16,0},{24,8},{32,48},{40,56},{48,32},{56,40},{64,80... | collective-permute-start | bytes 12582920 | tf_op jit(solution)/shard_map/ppermute | solution.py:52
  714.3 183.3 %copy-start.5 = (f32[2,2048,256]{2,1,0:T(8,128)S(1)}, f32[2,2048,256]{2,1,0:T(8,128)}, u32[]{:S(2)}) copy-start(f32[2,2048,256]{2,1,0:T(8,128)} %all-gather.6.cloned.1.call-done) | copy-start | bytes 12582916
  714.4 91.1 %collective-permute-start.6 = (f32[2,2048,256]{2,1,0:T(8,128)S(1)}, f32[2,2048,256]{2,1,0:T(8,128)S(1)}, u32[]{:S(2)}, u32[]{:S(2)}) collective-permute-start(f32[2,2048,256]{2,1,0:T(8,128)S(1)} %add.51), channel_id=1, source_target_pairs={{0,32},{8,40},{16,48},{24,56},{32,0},{40,8},{48,16},{56,24},{64,96... | collective-permute-start | bytes 12582920 | tf_op jit(solution)/shard_map/ppermute | solution.py:52
  806.0 91.7 %collective-permute-start.7 = (f32[2,2048,256]{2,1,0:T(8,128)S(1)}, f32[2,2048,256]{2,1,0:T(8,128)S(1)}, u32[]{:S(2)}, u32[]{:S(2)}) collective-permute-start(f32[2,2048,256]{2,1,0:T(8,128)S(1)} %add.52), channel_id=1, source_target_pairs={{0,64},{8,72},{16,80},{24,88},{32,96},{40,104},{48,112},{56,120},{... | collective-permute-start | bytes 12582920 | tf_op jit(solution)/shard_map/ppermute | solution.py:52
  908.7 3.5 copy-start.4
  912.3 36.6 %copy-start.7 = (f32[2,128,256]{2,1,0:T(8,128)S(1)}, f32[2,128,256]{2,1,0:T(8,128)}, u32[]{:S(2)}) copy-start(f32[2,128,256]{2,1,0:T(8,128)} %reduce-scatter.3.cloned.1.call-done) | copy-start | bytes 786436
Sparse Core Ops, SparseCore 0:
  11.1 25.6 all-gather.3
  459.5 33.6 reduce-scatter.2
  495.5 22.1 all-gather.7
  915.1 33.6 reduce-scatter.4
Sparse Core Ops, SparseCore 1:
  237.0 67.7 all-gather.5
